TPU v7x, 256 devices: a whole 4x4x8 slice. The times are simulated.
256 devices in a mesh: seq: 16 (over z, core), tp: 8 (over x_lo, y), dp: 2 (over x_hi).
Axes of the slice: x: 4 (x_hi: 2, x_lo: 2; x = x_hi * 2 + x_lo), y: 4, z: 8, core: 2. Of those that a mesh axis runs over, the one named last changes fastest.
Arguments:
- query_latent: bfloat16 [2, 4096, 1536], P('dp', 'seq', 'tp'), may hold values from -6 to 6
- key_latent: bfloat16 [2, 4096, 512], P('dp', 'seq', 'tp'), may hold values from -6 to 6
- rope_key: bfloat16 [2, 4096, 64], P('dp', 'seq'), may hold values from -6 to 6
- w_uq: bfloat16 [1536, 12288], P('seq', 'tp')
- w_uk: bfloat16 [512, 8192], P('seq', 'tp'), may hold values from -0.25 to 0.25
- w_uv: bfloat16 [512, 8192], P('seq', 'tp'), may hold values from -0.25 to 0.25
- block_order: int32 [2, 32], P('dp'), may hold values from 0 to 31, each once within a row
- segment_ids: int32 [2, 4096], P('dp'), may hold values from 0 to 3, never falling along the last dimension, each value on 1 to 2048 neighbouring positions
Outputs:
- context: bfloat16 [2, 4096, 8192], P('dp', 'seq', 'tp')
- clipped_uq: bfloat16 [1536, 12288], P('seq', 'tp')
- clipped_uk: bfloat16 [512, 8192], P('seq', 'tp')
Inputs may be any that keep to these rules, and one draw needn't show every extreme that they name: `block_order`: each row is a permutation of the 32 position blocks. `segment_ids`: never falling along positions; each document has at most 2048 positions.
All inputs are finite; a program needn't handle non-finite values.
Results may differ from a plain program's by a relative error of at most 0.012.
The roundings to bfloat16 on the way count: a program that leaves them out, or rounds other values in their place, can miss the bound.
Values may be sent and summed in bfloat16 or wider, within the bound.
A program may use at most 64 MiB of HBM per device.

v0:
```python
import math
import jax
import jax.numpy as jnp
from jax import lax
from jax.sharding import PartitionSpec as P

NOPE = 128
ROPE = 64
VD = 128
CLIP = 8
rope_base = 50000.0
masked_value = -1e30


def in_one_piece(arrays, axis, dim, along):
    both = jnp.concatenate(arrays, axis=along)
    whole, at, gathered = (lax.all_gather(both, axis, axis=dim, tiled=True), 0, [])
    for a in arrays:
        gathered.append(lax.slice_in_dim(whole, at, at + a.shape[along], axis=along))
        at += a.shape[along]
    return tuple(gathered)


def copy_for_each(array, axis):
    copies = jnp.broadcast_to(array, (lax.axis_size(axis), *array.shape))
    return lax.all_to_all(copies, axis, split_axis=0, concat_axis=0, tiled=True)


def of_everyone(array, axis):
    everything = copy_for_each(array, axis)
    return jnp.max(everything, axis=0)


def turning(positions, width):
    steps = jnp.arange(width // 2, dtype=jnp.float32) * (2.0 / width)
    freqs = jnp.exp(-math.log(rope_base) * steps)
    angle = positions.astype(jnp.float32)[:, None] * freqs[None, :]
    return (jnp.cos(angle), jnp.sin(angle))


def rotate(values, cosine, sine):
    half = values.shape[-1] // 2
    first = values[..., :half]
    second = values[..., half:]
    return jnp.concatenate(
        [first * cosine - second * sine, second * cosine + first * sine], axis=-1
    )


def positions_of(index, order, half_block):
    which = index // half_block
    onehot = which[:, None] == jnp.arange(order.shape[0], dtype=jnp.int32)[None, :]
    base = jnp.sum(jnp.where(onehot, order[None, :], 0), axis=1)
    return base * half_block + index % half_block


def on_device(query_latent, key_latent, rope_key, w_uq, w_uk, w_uv, block_order, segment_ids):
    query_local, key_local = (
        lax.all_gather(query_latent[0], "tp", axis=1, tiled=True),
        lax.all_gather(key_latent[0], "tp", axis=1, tiled=True),
    )
    rows_uq, rows_uk, rows_uv = (
        lax.all_gather(w_uq, "seq", axis=0, tiled=True),
        *in_one_piece((w_uk, w_uv), "seq", 0, 1),
    )
    tok_rows = query_local.shape[0]
    half_block = tok_rows // 2
    order = block_order[0]
    labels_all = segment_ids[0]
    heads = w_uq.shape[1] // (NOPE + ROPE)
    scale = 1.0 / math.sqrt(NOPE + ROPE)
    own_index = lax.axis_index("seq") * tok_rows + jnp.arange(tok_rows, dtype=jnp.int32)
    query_pos = positions_of(own_index, order, half_block)
    query_labels = jnp.take(labels_all, query_pos)
    cosine, sine = turning(query_pos, ROPE)
    query_full = jnp.dot(query_local, rows_uq, preferred_element_type=jnp.float32).reshape(
        tok_rows, heads, NOPE + ROPE
    )
    query_nope = jnp.transpose(query_full[:, :, :NOPE].astype(jnp.bfloat16), (1, 0, 2))
    query_rope = jnp.transpose(
        rotate(query_full[:, :, NOPE:], cosine[:, None, :], sine[:, None, :]).astype(jnp.bfloat16),
        (1, 0, 2),
    )
    key_rope = rotate(rope_key[0].astype(jnp.float32), cosine, sine).astype(jnp.bfloat16)

    def slice_latent(pieces, first, width):
        latent_block = lax.dynamic_slice_in_dim(pieces[0], first, width, 0)
        rope_block = lax.dynamic_slice_in_dim(pieces[1], first, width, 0)
        nope_block = jnp.dot(latent_block, rows_uk, preferred_element_type=jnp.float32).astype(
            jnp.bfloat16
        )
        value_block = jnp.dot(latent_block, rows_uv, preferred_element_type=jnp.float32).astype(
            jnp.bfloat16
        )
        return (nope_block, value_block, rope_block)

    initial = (
        jnp.full((heads, tok_rows), masked_value, jnp.float32),
        jnp.zeros((heads, tok_rows), jnp.float32),
        jnp.zeros((heads, tok_rows, VD), jnp.float32),
    )
    pieces = in_one_piece((key_local, key_rope), "seq", 0, 1)
    count = pieces[-1].shape[0]
    width = math.gcd(count, 512)

    def block_step(state, number):
        first = number * width
        nope_block, value_block, rope_block = slice_latent(pieces, first, width)
        nope_block = nope_block.reshape(width, heads, NOPE)
        value_block = value_block.reshape(width, heads, VD)
        key_index = first + jnp.arange(width, dtype=jnp.int32)
        key_pos = positions_of(key_index, order, half_block)
        key_labels = jnp.take(labels_all, key_pos)
        allowed = (key_pos[None, :] <= query_pos[:, None]) & (
            key_labels[None, :] == query_labels[:, None]
        )
        scores = jnp.einsum(
            "hqd,khd->hqk", query_nope, nope_block, preferred_element_type=jnp.float32
        )
        scores = (
            scores
            + jnp.einsum("hqr,kr->hqk", query_rope, rope_block, preferred_element_type=jnp.float32)
        ) * scale
        masked = jnp.where(allowed[None], scores, masked_value)
        run_max, run_total, run_sum = state
        new_max = jnp.maximum(run_max, jnp.max(masked, axis=2))
        weights = jnp.where(allowed[None], jnp.exp(masked - new_max[:, :, None]), 0.0)
        shrink = jnp.exp(run_max - new_max)
        new_total = run_total * shrink + jnp.sum(weights, axis=2)
        mixed = jnp.einsum(
            "hqk,khv->hqv",
            weights.astype(jnp.bfloat16),
            value_block,
            preferred_element_type=jnp.float32,
        )
        new_sum = run_sum * shrink[:, :, None] + mixed
        return ((new_max, new_total, new_sum), None)

    result, unused = lax.scan(block_step, initial, jnp.arange(count // width, dtype=jnp.int32))
    run_max, run_total, run_sum = result
    context = (run_sum / run_total[:, :, None]).astype(jnp.bfloat16)
    context = jnp.transpose(context, (1, 0, 2)).reshape(1, tok_rows, heads * VD)
    head_max = of_everyone(jnp.max(run_max, axis=1), ("seq", "dp"))
    ratio = CLIP / jnp.maximum(head_max, CLIP)
    root = jnp.sqrt(ratio)
    factors = jnp.concatenate(
        [
            jnp.broadcast_to(root[:, None], (heads, NOPE)),
            jnp.broadcast_to(ratio[:, None], (heads, ROPE)),
        ],
        axis=1,
    ).reshape(heads * (NOPE + ROPE))
    clipped_uq = (w_uq.astype(jnp.float32) * factors[None, :]).astype(jnp.bfloat16)
    clipped_uk = (w_uk.astype(jnp.float32) * jnp.repeat(root, NOPE)[None, :]).astype(jnp.bfloat16)
    return (context, clipped_uq, clipped_uk)


def solution(mesh):
    placed = (
        P("dp", "seq", "tp"),
        P("dp", "seq", "tp"),
        P("dp", "seq", None),
        P("seq", "tp"),
        P("seq", "tp"),
        P("seq", "tp"),
        P("dp", None),
        P("dp", None),
    )
    return jax.shard_map(
        on_device,
        mesh=mesh,
        in_specs=placed,
        out_specs=(P("dp", "seq", "tp"), P("seq", "tp"), P("seq", "tp")),
        check_vma=False,
    )
```

profile of v0, /device:TPU:1, one launch (start us, length us, event | category | flops | bytes accessed | tf_op | source)
XLA Modules:
  0.0 318.9 jit_solution(3619751761167049649)
XLA Ops:
  10.4 24.1 %all-gather = bf16[1,256,512]{1,2,0:T(8,128)(2,1)S(1)} all-gather(bf16[1,256,64]{1,2,0:T(8,128)(2,1)} %param.11), channel_id=2, replica_groups=mesh['seq'=16,'tp'=8,'dp'=2] {'tp'}, dimensions={2}, use_global_device_ids=true | all-gather | bytes 294912 | tf_op jit(solution)/shard_map/all_gather | solution.py:60
  38.2 24.7 %all-gather.1 = bf16[1,256,1536]{1,2,0:T(8,128)(2,1)S(1)} all-gather(bf16[1,256,192]{1,2,0:T(8,128)(2,1)} %param.10), channel_id=3, replica_groups=mesh['seq'=16,'tp'=8,'dp'=2] {'tp'}, dimensions={2}, use_global_device_ids=true | all-gather | bytes 884736 | tf_op jit(solution)/shard_map/all_gather | solution.py:59
  62.9 3.2 fusion.47
  66.0 30.5 %all-gather.10.cloned.1.call-done = bf16[1536,1536]{1,0:T(8,128)(2,1)} async-done(((bf16[96,1536]{1,0:T(8,128)(2,1)}), bf16[1536,1536]{1,0:T(8,128)(2,1)}) %all-gather.10.cloned.1.call-update) | async-done | bytes 4718608 | tf_op jit(solution)/shard_map/all_gather | solution.py:63
  96.5 4.3 %fusion.34 = f32[256,1536]{0,1:T(8,128)S(1)} fusion(bf16[1536,1536]{1,0:T(8,128)(2,1)} %all-gather.10.cloned.1.call-done, bf16[1,256,1536]{1,2,0:T(8,128)(2,1)S(1)} %all-gather.1), kind=kOutput, calls=%fused_computation.61 | convolution fusion | flops 1207959552 | bytes 7077888 | tf_op jit(solution)/shard_map/dot_general | solution.py:76
  103.5 46.1 %all-gather.6.cloned.1.call-done = bf16[4096,576]{0,1:T(8,128)(2,1)} async-done(((bf16[256,576]{0,1:T(8,128)(2,1)}), bf16[4096,576]{0,1:T(8,128)(2,1)}) %all-gather.6.cloned.1.call-update) | async-done | bytes 4718608 | tf_op jit(solution)/shard_map/all_gather | solution.py:17
  149.6 4.8 %slice.46 = bf16[4096,512]{0,1:T(8,128)(2,1)} slice(bf16[4096,576]{0,1:T(8,128)(2,1)} %all-gather.6.cloned.1.call-done), slice={[0:4096], [0:512]} | slice | bytes 8388608 | tf_op jit(solution)/shard_map/slice | solution.py:19
  154.4 139.5 %while.17 = (s32[]{:T(128)}, f32[8,256]{1,0:T(8,128)S(1)}, f32[8,256]{1,0:T(8,128)S(1)}, f32[8,256,128]{2,1,0:T(8,128)S(1)}, s32[8]{0:T(128)S(1)}, /*index=5*/s3...) while((s32[]{:T(128)}, f32[8,256]{1,0:T(8,128)S(1)}, ...), condition=%wide.region_5.6_spmd.clone, body=%wide.region_1.5_spmd.clone.sunk | while | flops 1757632000 | bytes 48734628 | solution.py:139
  155.8 3.1 gather_fusion
  165.0 3.1 fusion.81
  173.2 3.1 gather_fusion
  182.4 3.1 fusion.81
  190.7 3.1 gather_fusion
  199.9 3.1 fusion.81
  208.1 3.1 gather_fusion
  217.3 3.1 fusion.81
  225.6 3.1 gather_fusion
  234.8 3.1 fusion.81
  243.0 3.1 gather_fusion
  252.2 3.1 fusion.81
  260.4 3.1 gather_fusion
  277.9 3.1 gather_fusion
  294.7 6.6 %all-to-all-start = ((f32[32,1,8]{2,1,0:T(1,128)}), f32[32,1,8]{2,1,0:T(1,128)S(1)}, u32[]{:S(2)}, u32[]{:S(2)}) async-start(f32[32,1,8]{2,1,0:T(1,128)} %broadcast_in_dim.126), calls=%async_computation | async-start | bytes 32768 | tf_op jit(solution)/shard_map/all_to_all | solution.py:26
  303.0 7.6 %all-to-all-done = f32[32,1,8]{2,1,0:T(1,128)S(1)} async-done(((f32[32,1,8]{2,1,0:T(1,128)}), f32[32,1,8]{2,1,0:T(1,128)S(1)}, u32[]{:S(2)}, u32[]{:S(2)}) %all-to-all-start) | async-done | bytes 1056 | tf_op jit(solution)/shard_map/all_to_all | solution.py:26
  (199 shorter events, 103.6 us)
Async XLA Ops:
  7.2 55.7 %all-gather.8.cloned.1.call-start = ((), (), s32[]{:S(2)}) async-start(), calls=%async_computation.2 | async-start | bytes 2228224 | tf_op jit(solution)/shard_map/all_gather | solution.py:17
  8.8 87.7 %all-gather.10.cloned.1.call-start = ((), (), s32[]{:S(2)}) async-start(), calls=%async_computation.3 | async-start | bytes 5013504 | tf_op jit(solution)/shard_map/all_gather | solution.py:63
  9.5 140.1 %all-gather.6.cloned.1.call-start = ((), (), s32[]{:S(2)}) async-start(), calls=%async_computation.1 | async-start | bytes 5013504 | tf_op jit(solution)/shard_map/all_gather | solution.py:17
  100.8 1.2 copy-start.3
  103.4 50.9 %copy-start = (s32[1,4096]{1,0:T(1,128)S(1)}, s32[1,4096]{1,0:T(1,128)}, u32[]{:S(2)}) copy-start(s32[1,4096]{1,0:T(1,128)} %param.17) | copy-start | bytes 49156
  103.4 50.9 %copy-start.5 = (s32[1,32]{1,0:T(1,128)S(1)}, s32[1,32]{1,0:T(1,128)}, u32[]{:S(2)}) copy-start(s32[1,32]{1,0:T(1,128)} %param.16) | copy-start | bytes 388
  149.6 4.8 %slice-start = ((bf16[4096,576]{0,1:T(8,128)(2,1)}), bf16[4096,64]{0,1:T(8,128)(2,1)S(1)}, s32[]{:S(2)}) async-start(bf16[4096,576]{0,1:T(8,128)(2,1)} %all-gather.6.cloned.1.call-done), calls=%async_computation.4 | async-start | bytes 1048576 | tf_op jit(solution)/shard_map/slice | solution.py:19
  154.4 156.6 %copy-start.2 = (bf16[96,1536]{1,0:T(8,128)(2,1)S(1)}, bf16[96,1536]{1,0:T(8,128)(2,1)}, u32[]{:S(2)}) copy-start(bf16[96,1536]{1,0:T(8,128)(2,1)} %param.13) | copy-start | bytes 884740
  165.0 5.2 %copy-start.1 = (f32[8,256,512]{1,2,0:T(8,128)S(1)}, f32[8,256,512]{1,2,0:T(8,128)}, u32[]{:S(2)}) copy-start(f32[8,256,512]{1,2,0:T(8,128)} %get-tuple-element.455) | copy-start | bytes 12582916 | tf_op jit(solution)/shard_map/while
  182.4 5.2 %copy-start.1 = (f32[8,256,512]{1,2,0:T(8,128)S(1)}, f32[8,256,512]{1,2,0:T(8,128)}, u32[]{:S(2)}) copy-start(f32[8,256,512]{1,2,0:T(8,128)} %get-tuple-element.455) | copy-start | bytes 12582916 | tf_op jit(solution)/shard_map/while
  199.9 5.2 %copy-start.1 = (f32[8,256,512]{1,2,0:T(8,128)S(1)}, f32[8,256,512]{1,2,0:T(8,128)}, u32[]{:S(2)}) copy-start(f32[8,256,512]{1,2,0:T(8,128)} %get-tuple-element.455) | copy-start | bytes 12582916 | tf_op jit(solution)/shard_map/while
  217.3 5.2 %copy-start.1 = (f32[8,256,512]{1,2,0:T(8,128)S(1)}, f32[8,256,512]{1,2,0:T(8,128)}, u32[]{:S(2)}) copy-start(f32[8,256,512]{1,2,0:T(8,128)} %get-tuple-element.455) | copy-start | bytes 12582916 | tf_op jit(solution)/shard_map/while
  234.8 5.2 %copy-start.1 = (f32[8,256,512]{1,2,0:T(8,128)S(1)}, f32[8,256,512]{1,2,0:T(8,128)}, u32[]{:S(2)}) copy-start(f32[8,256,512]{1,2,0:T(8,128)} %get-tuple-element.455) | copy-start | bytes 12582916 | tf_op jit(solution)/shard_map/while
  252.2 5.2 %copy-start.1 = (f32[8,256,512]{1,2,0:T(8,128)S(1)}, f32[8,256,512]{1,2,0:T(8,128)}, u32[]{:S(2)}) copy-start(f32[8,256,512]{1,2,0:T(8,128)} %get-tuple-element.455) | copy-start | bytes 12582916 | tf_op jit(solution)/shard_map/while
  269.6 5.2 %copy-start.1 = (f32[8,256,512]{1,2,0:T(8,128)S(1)}, f32[8,256,512]{1,2,0:T(8,128)}, u32[]{:S(2)}) copy-start(f32[8,256,512]{1,2,0:T(8,128)} %get-tuple-element.455) | copy-start | bytes 12582916 | tf_op jit(solution)/shard_map/while
  287.1 5.2 %copy-start.1 = (f32[8,256,512]{1,2,0:T(8,128)S(1)}, f32[8,256,512]{1,2,0:T(8,128)}, u32[]{:S(2)}) copy-start(f32[8,256,512]{1,2,0:T(8,128)} %get-tuple-element.455) | copy-start | bytes 12582916 | tf_op jit(solution)/shard_map/while
  293.9 17.8 %copy-start.4 = (bf16[32,1024]{1,0:T(8,128)(2,1)S(1)}, bf16[32,1024]{1,0:T(8,128)(2,1)}, u32[]{:S(2)}) copy-start(bf16[32,1024]{1,0:T(8,128)(2,1)} %param.14) | copy-start | bytes 196612
  294.7 15.9 %all-to-all-start = ((f32[32,1,8]{2,1,0:T(1,128)}), f32[32,1,8]{2,1,0:T(1,128)S(1)}, u32[]{:S(2)}, u32[]{:S(2)}) async-start(f32[32,1,8]{2,1,0:T(1,128)} %broadcast_in_dim.126), calls=%async_computation | async-start | bytes 32768 | tf_op jit(solution)/shard_map/all_to_all | solution.py:26
Sparse Core Ops, SparseCore 0:
  10.4 43.6 all-gather.7
  55.9 40.5 all-gather.9
  98.8 50.7 all-gather.5
where the time goes:
time: 320 us; the launch traced here: 319 us
  waiting for transfers between devices  84.9 us (27%)
  matrix products  80.3 us (25%)
  blocking collectives  48.7 us (15%)
  local copies, waits for them, and re-layouts  43.6 us (14%)
  other arithmetic  34.6 us (11%)
  between operations  13.9 us (4%)
  starting transfers between devices  6.74 us (2%)
  loops' own time  6.11 us (2%)
    all_gather x2, waiting for transfers between devices, in_one_piece(): lax.all_gather(both, axis, axis=dim, tiled=True)  46.1 us
    all_gather x1, waiting for transfers between devices, on_device(): lax.all_gather(w_uq, 'seq', axis=0, tiled=True)  30.5 us
    gather x8, local copies, waits for them, and re-layouts, block_step(): key_labels = jnp.take(labels_all, key_pos)  25.1 us
    all_gather x1, blocking collectives, on_device(): lax.all_gather(query_latent[0], 'tp', axis=1, tiled=True)  24.7 us
    reduce_sum x8, other arithmetic, block_step(): new_total = run_total * shrink + jnp.sum(weights, axis=2)  24.5 us
    all_gather x1, blocking collectives, on_device(): lax.all_gather(key_latent[0], 'tp', axis=1, tiled=True)  24.1 us
    dot_general x8, matrix products, block_step(): jnp.einsum('hqr,kr->hqk', query_rope, rope_block, preferred_element_type=...  23.8 us
    dot_general x8, matrix products, slice_latent(): jnp.dot(latent_block, rows_uv, preferred_element_type=jnp.float32)  17 us
  transfers between devices with their start and end apart: 4, of which 3 were waited for; matrix products, arithmetic and copies ran while one was open for 5% of the time, Pallas kernels for 0%

commit v1 on v0

--- a/solution.py
+++ b/solution.py
@@ -3,6 +3,7 @@
 import jax.numpy as jnp
 from jax import lax
 from jax.sharding import PartitionSpec as P
+from jax.lax import all_to_all, axis_size
 
 NOPE = 128
 ROPE = 64
@@ -55,14 +56,16 @@
 
 
 def on_device(query_latent, key_latent, rope_key, w_uq, w_uk, w_uv, block_order, segment_ids):
+
+    def resolve_the_ways(work_x):
+        a_now = jnp.concatenate(axis_size("seq") * [work_x], axis=0)
+        return all_to_all(a_now, "seq", 0, 0, tiled=True)
+
     query_local, key_local = (
         lax.all_gather(query_latent[0], "tp", axis=1, tiled=True),
         lax.all_gather(key_latent[0], "tp", axis=1, tiled=True),
     )
-    rows_uq, rows_uk, rows_uv = (
-        lax.all_gather(w_uq, "seq", axis=0, tiled=True),
-        *in_one_piece((w_uk, w_uv), "seq", 0, 1),
-    )
+    rows_uq, rows_uk, rows_uv = (resolve_the_ways(w_uq), *in_one_piece((w_uk, w_uv), "seq", 0, 1))
     tok_rows = query_local.shape[0]
     half_block = tok_rows // 2
     order = block_order[0]

time: 320 us -> 344 us (1.075)
  starting transfers between devices: 6.74 us -> 17.4 us
  local copies, waits for them, and re-layouts: 43.6 us -> 52.5 us
    all_to_all x0 -> x1, waiting for transfers between devices: none -> 59.6 us  [resolve_the_ways(): return all_to_all(a_now, 'seq', 0, 0, tiled=True)]
    all_gather x1 -> x0, waiting for transfers between devices: 30.5 us -> none  [on_device(): lax.all_gather(w_uq, 'seq', axis=0, tiled=True)]
    all_gather x2, waiting for transfers between devices: 46.1 us -> 20.6 us  [in_one_piece(): lax.all_gather(both, axis, axis=dim, tiled=True)]
    all_to_all x0 -> x1, starting transfers between devices: none -> 10.1 us  [resolve_the_ways(): return all_to_all(a_now, 'seq', 0, 0, tiled=True)]
    unnamed x11 -> x34, local copies, waits for them, and re-layouts: 1.46 us -> 10.7 us
  transfers between devices with their start and end apart: 4 -> 4, of which waited for: 3 -> 4; matrix products, arithmetic and copies ran while one was open for 5% -> 6% of each run, Pallas kernels for 0% -> 0%
where the time goes in v1:
time: 344 us; the launch traced here: 343 us
  waiting for transfers between devices  87.8 us (26%)
  matrix products  79.8 us (23%)
  local copies, waits for them, and re-layouts  52.5 us (15%)
  blocking collectives  51.4 us (15%)
  other arithmetic  33.2 us (10%)
  starting transfers between devices  17.4 us (5%)
  between operations  14.4 us (4%)
  loops' own time  6.1 us (2%)
    all_to_all x1, waiting for transfers between devices, resolve_the_ways(): return all_to_all(a_now, 'seq', 0, 0, tiled=True)  59.6 us
    all_gather x1, blocking collectives, on_device(): lax.all_gather(query_latent[0], 'tp', axis=1, tiled=True)  26 us
    all_gather x1, blocking collectives, on_device(): lax.all_gather(key_latent[0], 'tp', axis=1, tiled=True)  25.4 us
    gather x8, local copies, waits for them, and re-layouts, block_step(): key_labels = jnp.take(labels_all, key_pos)  25.1 us
    reduce_sum x8, other arithmetic, block_step(): new_total = run_total * shrink + jnp.sum(weights, axis=2)  24.5 us
    dot_general x8, matrix products, block_step(): jnp.einsum('hqr,kr->hqk', query_rope, rope_block, preferred_element_type=...  23.8 us
    all_gather x2, waiting for transfers between devices, in_one_piece(): lax.all_gather(both, axis, axis=dim, tiled=True)  20.6 us
    dot_general x8, matrix products, slice_latent(): jnp.dot(latent_block, rows_uv, preferred_element_type=jnp.float32)  17 us
  transfers between devices with their start and end apart: 4, of which 4 were waited for; matrix products, arithmetic and copies ran while one was open for 6% of the time, Pallas kernels for 0%

profile of v1, /device:TPU:1, one launch (start us, length us, event | category | flops | bytes accessed | tf_op | source)
XLA Modules:
  0.0 342.7 jit_solution(14988081886214848970)
XLA Ops:
  18.2 10.1 %all-to-all-start = ((bf16[16,96,1536]{2,1,0:T(8,128)(2,1)}), bf16[16,96,1536]{2,1,0:T(8,128)(2,1)}, u32[]{:S(2)}, u32[]{:S(2)}) async-start(bf16[16,96,1536]{2,1,0:T(8,128)(2,1)} %bitcast.84), calls=%async_computation | async-start | bytes 9437184 | tf_op jit(solution)/shard_map/all_to_all | solution.py:62
  28.5 25.4 %all-gather = bf16[1,256,512]{1,2,0:T(8,128)(2,1)S(1)} all-gather(bf16[1,256,64]{1,2,0:T(8,128)(2,1)S(1)} %copy-done.7), channel_id=2, replica_groups=mesh['seq'=16,'tp'=8,'dp'=2] {'tp'}, dimensions={2}, use_global_device_ids=true | all-gather | bytes 294912 | tf_op jit(solution)/shard_map/all_gather | solution.py:66
  56.8 26.0 %all-gather.1 = bf16[1,256,1536]{1,2,0:T(8,128)(2,1)S(1)} all-gather(bf16[1,256,192]{1,2,0:T(8,128)(2,1)S(1)} %copy-done.6), channel_id=3, replica_groups=mesh['seq'=16,'tp'=8,'dp'=2] {'tp'}, dimensions={2}, use_global_device_ids=true | all-gather | bytes 884736 | tf_op jit(solution)/shard_map/all_gather | solution.py:65
  82.8 5.4 %all-gather.7.cloned.1.call-done = bf16[512,2048]{1,0:T(8,128)(2,1)} async-done(((bf16[32,2048]{1,0:T(8,128)(2,1)}), bf16[512,2048]{1,0:T(8,128)(2,1)}) %all-gather.7.cloned.1.call-update) | async-done | bytes 2097168 | tf_op jit(solution)/shard_map/all_gather | solution.py:18
  91.2 59.6 %all-to-all-done = bf16[16,96,1536]{2,1,0:T(8,128)(2,1)} async-done(((bf16[16,96,1536]{2,1,0:T(8,128)(2,1)}), bf16[16,96,1536]{2,1,0:T(8,128)(2,1)}, u32[]{:S(2)}, u32[]{:S(2)}) %all-to-all-start) | async-done | bytes 4718624 | tf_op jit(solution)/shard_map/all_to_all | solution.py:62
  150.8 3.8 %fusion.34 = f32[1536,256]{1,0:T(8,128)S(1)} fusion(bf16[1536,1536]{1,0:T(8,128)(2,1)} %bitcast.8, bf16[1,256,1536]{1,2,0:T(8,128)(2,1)S(1)} %all-gather.1), kind=kOutput, calls=%fused_computation.61 | convolution fusion | flops 1207959552 | bytes 7077888 | tf_op jit(solution)/shard_map/dot_general | solution.py:79
  157.3 15.3 %all-gather.5.cloned.1.call-done = bf16[4096,576]{0,1:T(8,128)(2,1)} async-done(((bf16[256,576]{0,1:T(8,128)(2,1)}), bf16[4096,576]{0,1:T(8,128)(2,1)}) %all-gather.5.cloned.1.call-update) | async-done | bytes 4718608 | tf_op jit(solution)/shard_map/all_gather | solution.py:18
  172.6 4.8 %slice.46 = bf16[4096,512]{0,1:T(8,128)(2,1)} slice(bf16[4096,576]{0,1:T(8,128)(2,1)} %all-gather.5.cloned.1.call-done), slice={[0:4096], [0:512]} | slice | bytes 8388608 | tf_op jit(solution)/shard_map/slice | solution.py:20
  177.4 139.5 %while.17 = (s32[]{:T(128)}, f32[8,256]{1,0:T(8,128)S(1)}, f32[8,256]{1,0:T(8,128)S(1)}, f32[8,256,128]{2,1,0:T(8,128)S(1)}, s32[8]{0:T(128)S(1)}, /*index=5*/s3...) while((s32[]{:T(128)}, f32[8,256]{1,0:T(8,128)S(1)}, ...), condition=%wide.region_5.6_spmd.clone, body=%wide.region_1.5_spmd.clone.sunk | while | flops 1757632000 | bytes 48734628 | solution.py:142
  178.7 3.1 gather_fusion
  188.0 3.1 fusion.81
  196.2 3.1 gather_fusion
  205.4 3.1 fusion.81
  213.6 3.1 gather_fusion
  222.8 3.1 fusion.81
  231.1 3.1 gather_fusion
  240.3 3.1 fusion.81
  248.5 3.1 gather_fusion
  257.7 3.1 fusion.81
  265.9 3.1 gather_fusion
  283.4 3.1 gather_fusion
  300.8 3.1 gather_fusion
  317.6 7.2 %all-to-all-start.1 = ((f32[32,1,8]{2,1,0:T(1,128)}), f32[32,1,8]{2,1,0:T(1,128)S(1)}, u32[]{:S(2)}, u32[]{:S(2)}) async-start(f32[32,1,8]{2,1,0:T(1,128)} %broadcast_in_dim.126), calls=%async_computation.1 | async-start | bytes 32768 | tf_op jit(solution)/shard_map/all_to_all | solution.py:27
  326.5 7.6 %all-to-all-done.1 = f32[32,1,8]{2,1,0:T(1,128)S(1)} async-done(((f32[32,1,8]{2,1,0:T(1,128)}), f32[32,1,8]{2,1,0:T(1,128)S(1)}, u32[]{:S(2)}, u32[]{:S(2)}) %all-to-all-start.1) | async-done | bytes 1056 | tf_op jit(solution)/shard_map/all_to_all | solution.py:27
  (222 shorter events, 116.6 us)
Async XLA Ops:
  7.2 8.6 %copy-start.2 = (bf16[96,1536]{1,0:T(8,128)(2,1)S(1)}, bf16[96,1536]{1,0:T(8,128)(2,1)}, u32[]{:S(2)}) copy-start(bf16[96,1536]{1,0:T(8,128)(2,1)} %param.13) | copy-start | bytes 884740
  7.2 81.0 %all-gather.7.cloned.1.call-start = ((), (), s32[]{:S(2)}) async-start(), calls=%async_computation.3 | async-start | bytes 2228224 | tf_op jit(solution)/shard_map/all_gather | solution.py:18
  16.0 2.2 copy-start.3
  18.2 10.2 %copy-start.9 = (s32[1,32]{1,0:T(1,128)S(1)}, s32[1,32]{1,0:T(1,128)}, u32[]{:S(2)}) copy-start(s32[1,32]{1,0:T(1,128)} %param.16) | copy-start | bytes 388
  18.2 10.3 %copy-start.7 = (bf16[1,256,64]{1,2,0:T(8,128)(2,1)S(1)}, bf16[1,256,64]{1,2,0:T(8,128)(2,1)}, u32[]{:S(2)}) copy-start(bf16[1,256,64]{1,2,0:T(8,128)(2,1)} %param.11) | copy-start | bytes 98308
  18.2 35.7 %copy-start.8 = (bf16[1,256,64]{1,2,0:T(8,128)(2,1)S(1)}, bf16[1,256,64]{1,2,0:T(8,128)(2,1)}, u32[]{:S(2)}) copy-start(bf16[1,256,64]{1,2,0:T(8,128)(2,1)} %param.12) | copy-start | bytes 98308
  18.2 36.8 %copy-start = (s32[1,4096]{1,0:T(1,128)S(1)}, s32[1,4096]{1,0:T(1,128)}, u32[]{:S(2)}) copy-start(s32[1,4096]{1,0:T(1,128)} %param.17) | copy-start | bytes 49156
  18.2 38.5 %copy-start.6 = (bf16[1,256,192]{1,2,0:T(8,128)(2,1)S(1)}, bf16[1,256,192]{1,2,0:T(8,128)(2,1)}, u32[]{:S(2)}) copy-start(bf16[1,256,192]{1,2,0:T(8,128)(2,1)} %param.10) | copy-start | bytes 294916
  18.2 132.6 %all-to-all-start = ((bf16[16,96,1536]{2,1,0:T(8,128)(2,1)}), bf16[16,96,1536]{2,1,0:T(8,128)(2,1)}, u32[]{:S(2)}, u32[]{:S(2)}) async-start(bf16[16,96,1536]{2,1,0:T(8,128)(2,1)} %bitcast.84), calls=%async_computation | async-start | bytes 9437184 | tf_op jit(solution)/shard_map/all_to_all | solution.py:62
  28.4 144.2 %all-gather.5.cloned.1.call-start = ((), (), s32[]{:S(2)}) async-start(), calls=%async_computation.2 | async-start | bytes 5013504 | tf_op jit(solution)/shard_map/all_gather | solution.py:18
  154.7 1.2 copy-start.4
  172.6 4.8 %slice-start = ((bf16[4096,576]{0,1:T(8,128)(2,1)}), bf16[4096,64]{0,1:T(8,128)(2,1)S(1)}, s32[]{:S(2)}) async-start(bf16[4096,576]{0,1:T(8,128)(2,1)} %all-gather.5.cloned.1.call-done), calls=%async_computation.4 | async-start | bytes 1048576 | tf_op jit(solution)/shard_map/slice | solution.py:20
  177.3 157.8 %copy-start.5 = (bf16[32,1024]{1,0:T(8,128)(2,1)S(1)}, bf16[32,1024]{1,0:T(8,128)(2,1)}, u32[]{:S(2)}) copy-start(bf16[32,1024]{1,0:T(8,128)(2,1)} %param.14) | copy-start | bytes 196612
  188.0 5.2 %copy-start.1 = (f32[8,256,512]{1,2,0:T(8,128)S(1)}, f32[8,256,512]{1,2,0:T(8,128)}, u32[]{:S(2)}) copy-start(f32[8,256,512]{1,2,0:T(8,128)} %get-tuple-element.455) | copy-start | bytes 12582916 | tf_op jit(solution)/shard_map/while
  205.4 5.2 %copy-start.1 = (f32[8,256,512]{1,2,0:T(8,128)S(1)}, f32[8,256,512]{1,2,0:T(8,128)}, u32[]{:S(2)}) copy-start(f32[8,256,512]{1,2,0:T(8,128)} %get-tuple-element.455) | copy-start | bytes 12582916 | tf_op jit(solution)/shard_map/while
  222.8 5.2 %copy-start.1 = (f32[8,256,512]{1,2,0:T(8,128)S(1)}, f32[8,256,512]{1,2,0:T(8,128)}, u32[]{:S(2)}) copy-start(f32[8,256,512]{1,2,0:T(8,128)} %get-tuple-element.455) | copy-start | bytes 12582916 | tf_op jit(solution)/shard_map/while
  240.3 5.2 %copy-start.1 = (f32[8,256,512]{1,2,0:T(8,128)S(1)}, f32[8,256,512]{1,2,0:T(8,128)}, u32[]{:S(2)}) copy-start(f32[8,256,512]{1,2,0:T(8,128)} %get-tuple-element.455) | copy-start | bytes 12582916 | tf_op jit(solution)/shard_map/while
  257.7 5.2 %copy-start.1 = (f32[8,256,512]{1,2,0:T(8,128)S(1)}, f32[8,256,512]{1,2,0:T(8,128)}, u32[]{:S(2)}) copy-start(f32[8,256,512]{1,2,0:T(8,128)} %get-tuple-element.455) | copy-start | bytes 12582916 | tf_op jit(solution)/shard_map/while
  275.1 5.2 %copy-start.1 = (f32[8,256,512]{1,2,0:T(8,128)S(1)}, f32[8,256,512]{1,2,0:T(8,128)}, u32[]{:S(2)}) copy-start(f32[8,256,512]{1,2,0:T(8,128)} %get-tuple-element.455) | copy-start | bytes 12582916 | tf_op jit(solution)/shard_map/while
  292.6 5.2 %copy-start.1 = (f32[8,256,512]{1,2,0:T(8,128)S(1)}, f32[8,256,512]{1,2,0:T(8,128)}, u32[]{:S(2)}) copy-start(f32[8,256,512]{1,2,0:T(8,128)} %get-tuple-element.455) | copy-start | bytes 12582916 | tf_op jit(solution)/shard_map/while
  310.0 5.2 %copy-start.1 = (f32[8,256,512]{1,2,0:T(8,128)S(1)}, f32[8,256,512]{1,2,0:T(8,128)}, u32[]{:S(2)}) copy-start(f32[8,256,512]{1,2,0:T(8,128)} %get-tuple-element.455) | copy-start | bytes 12582916 | tf_op jit(solution)/shard_map/while
  317.6 16.5 %all-to-all-start.1 = ((f32[32,1,8]{2,1,0:T(1,128)}), f32[32,1,8]{2,1,0:T(1,128)S(1)}, u32[]{:S(2)}, u32[]{:S(2)}) async-start(f32[32,1,8]{2,1,0:T(1,128)} %broadcast_in_dim.126), calls=%async_computation.1 | async-start | bytes 32768 | tf_op jit(solution)/shard_map/all_to_all | solution.py:27
Sparse Core Ops, SparseCore 0:
  10.4 77.7 all-gather.6
  90.5 82.0 all-gather.4
